TPU v7x, 32 devices: a whole 2x2x4 slice. The times are simulated.
32 devices in a mesh: replica: 2 (over core), fsdp: 16 (over z, y, x).
Axes of the slice: x: 2, y: 2, z: 4, core: 2. Of those that a mesh axis runs over, the one named last changes fastest.
Arguments:
- activations: bfloat16 [16384, 4096], P(('replica', 'fsdp')), may hold values from -6 to 6
- queries: bfloat16 [16384, 2048], P(('replica', 'fsdp')), may hold values from -60 to 60
- out_grad: bfloat16 [16384, 2048], P(('replica', 'fsdp')), may hold values from -6 to 6
- lengths: int32 [64], P(('replica', 'fsdp')), may hold values from 32 to 256
- norm_gain: float32 [4096], replicated, may hold values from 0.5 to 7
- key_master: float32 [4096, 512], P('fsdp'), may hold values from -0.09375 to 0.09375
- value_master: float32 [4096, 512], P('fsdp'), may hold values from -0.09375 to 0.09375
Outputs:
- key_direction: float32 [4096, 512], P('fsdp')
- value_direction: float32 [4096, 512], P('fsdp')
All inputs are finite; a program needn't handle non-finite values.
Results may differ from a plain program's by a relative error of at most 0.009.
The roundings to bfloat16 on the way count: a program that leaves them out, or rounds other values in their place, can miss the bound.
Values may be sent and summed in bfloat16 or wider, within the bound.
A program may use at most 128 MiB of HBM per device.

v0:
```python
import jax
import jax.numpy as jnp
from jax import lax
from jax.sharding import PartitionSpec as P

D = 4096
HD = 128
KVH = 4
GROUP = 4
LEN = 256


def attend(query_seq, key_seq, value_seq, grad_seq, length):
    scale_factor = 1.0 / HD**0.5
    positions = jnp.arange(LEN, dtype=jnp.int32)
    allowed = (positions[None, :] <= positions[:, None]) & (positions[None, :] < length)
    query_float = query_seq.astype(jnp.float32).reshape(LEN, KVH, GROUP, HD)
    key_float = key_seq.astype(jnp.float32).reshape(LEN, KVH, HD)
    value_float = value_seq.astype(jnp.float32).reshape(LEN, KVH, HD)
    scores = jnp.einsum("qhgd,khd->hgqk", query_float, key_float) * scale_factor
    scores = jnp.where(allowed[None, None], scores, jnp.float32(-1e30))
    row_peak = jnp.max(scores, axis=-1, keepdims=True)
    exponent = jnp.exp(scores - row_peak)
    probs = exponent / jnp.sum(exponent, axis=-1, keepdims=True)
    probs_low = lax.optimization_barrier(probs.astype(jnp.bfloat16))
    probs_back = probs_low.astype(jnp.float32)
    attended = jnp.einsum("hgqk,khd->qhgd", probs_back, value_float).astype(jnp.bfloat16)
    attended = lax.optimization_barrier(attended).astype(jnp.float32)
    live_rows = (positions < length).astype(jnp.float32)
    grad_float = (
        grad_seq.astype(jnp.float32).reshape(LEN, KVH, GROUP, HD) * live_rows[:, None, None, None]
    )
    row_delta = jnp.transpose(jnp.sum(grad_float * attended, axis=-1), (1, 2, 0))[..., None]
    value_grad = jnp.einsum("hgqk,qhgd->khd", probs_back, grad_float).astype(jnp.bfloat16)
    prob_grad = jnp.einsum("qhgd,khd->hgqk", grad_float, value_float)
    score_grad = lax.optimization_barrier((probs * (prob_grad - row_delta)).astype(jnp.bfloat16))
    key_grad = (
        jnp.einsum("hgqk,qhgd->khd", score_grad.astype(jnp.float32), query_float) * scale_factor
    ).astype(jnp.bfloat16)
    return (key_grad.reshape(LEN, KVH * HD), value_grad.reshape(LEN, KVH * HD))


def transposed_product(columns, combined):
    return lax.dot_general(
        columns, combined, (((0,), (0,)), ((), ())), preferred_element_type=jnp.float32
    )


def local(activations, queries, out_grad, lengths, norm_gain, key_master, value_master):
    tok_rows = activations.shape[0]
    width = key_master.shape[1]
    shard_rows = key_master.shape[0]
    act_float = activations.astype(jnp.float32)
    inverse = lax.rsqrt(jnp.mean(act_float * act_float, axis=-1, keepdims=True) + 1e-05)
    normed = (act_float * inverse * norm_gain[None, :]).astype(jnp.bfloat16)
    columns = normed
    key_sum = jnp.dot(
        columns,
        lax.all_gather(key_master.astype(jnp.bfloat16), "fsdp", axis=0, tiled=True),
        preferred_element_type=jnp.float32,
    )
    value_sum = jnp.dot(
        columns,
        lax.all_gather(value_master.astype(jnp.bfloat16), "fsdp", axis=0, tiled=True),
        preferred_element_type=jnp.float32,
    )
    key_proj = key_sum.astype(jnp.bfloat16)
    value_proj = value_sum.astype(jnp.bfloat16)
    seq_count = lengths.shape[0]
    qwidth = queries.shape[1]

    def one_seq(packed):
        return attend(packed[0], packed[1], packed[2], packed[3], packed[4])

    key_grad, value_grad = lax.map(
        one_seq,
        (
            queries.reshape(seq_count, LEN, qwidth),
            key_proj.reshape(seq_count, LEN, width),
            value_proj.reshape(seq_count, LEN, width),
            out_grad.reshape(seq_count, LEN, qwidth),
            lengths,
        ),
    )
    combined = jnp.concatenate(
        [key_grad.reshape(tok_rows, width), value_grad.reshape(tok_rows, width)], axis=1
    )
    replicas = lax.axis_size("replica")
    shards = lax.axis_size("fsdp")
    piece_rows = shard_rows // replicas
    permuted = (
        normed.reshape(tok_rows, shards, replicas, piece_rows)
        .transpose(0, 2, 1, 3)
        .reshape(tok_rows, shards * shard_rows)
    )
    columns = permuted
    owned_grad = lax.psum_scatter(
        transposed_product(columns, combined), ("replica", "fsdp"), scatter_dimension=0, tiled=True
    )
    total_sq = lax.psum(jnp.sum(owned_grad * owned_grad), ("replica", "fsdp"))
    summed = lax.all_gather(owned_grad.astype(jnp.bfloat16), "replica", axis=0, tiled=True).astype(
        owned_grad.dtype
    )
    unit_scale = jnp.sqrt(jnp.float32(2 * D * width)) / jnp.sqrt(total_sq + 1e-06)
    return (unit_scale * summed[:, :width], unit_scale * summed[:, width:])


def solution(mesh):
    in_specs = (
        P(("replica", "fsdp"), None),
        P(("replica", "fsdp"), None),
        P(("replica", "fsdp"), None),
        P(("replica", "fsdp")),
        P(),
        P("fsdp", None),
        P("fsdp", None),
    )
    out_specs = (P("fsdp", None), P("fsdp", None))
    return jax.shard_map(local, mesh=mesh, in_specs=in_specs, out_specs=out_specs, check_vma=False)
```

profile of v0, /device:TPU:7, one launch (start us, length us, event | category | flops | bytes accessed | tf_op | source)
XLA Modules:
  0.0 638.2 jit_solution(8576653580051986996)
XLA Ops:
  7.2 1.8 convert_element_type.74
  9.1 1.8 convert_element_type.72
  11.0 6.5 %copy.41 = bf16[512,4096]{0,1:T(8,128)(2,1)} copy(bf16[512,4096]{1,0:T(8,128)(2,1)} %param.9) | data formatting | bytes 8388608 | tf_op args[0]
  17.4 3.3 fusion.24
  21.0 1.1 fusion.26
  22.1 1.9 copy-done.2
  24.0 2.4 copy.42
  26.4 58.6 %all-gather.5.cloned.1.call-done = bf16[4096,512]{1,0:T(8,128)(2,1)} async-done(((bf16[256,512]{1,0:T(8,128)(2,1)}), bf16[4096,512]{1,0:T(8,128)(2,1)}) %all-gather.5.cloned.1.call-update) | async-done | bytes 4194320 | tf_op jit(solution)/shard_map/all_gather | solution.py:64
  85.0 5.8 convolution_convert_fusion.1
  90.8 71.2 %all-gather.3.cloned.1.call-done = bf16[4096,512]{1,0:T(8,128)(2,1)} async-done(((bf16[256,512]{1,0:T(8,128)(2,1)}), bf16[4096,512]{1,0:T(8,128)(2,1)}) %all-gather.3.cloned.1.call-update) | async-done | bytes 4194320 | tf_op jit(solution)/shard_map/all_gather | solution.py:59
  162.0 6.6 %convolution_convert_fusion.2 = bf16[512,512]{1,0:T(8,128)(2,1)} fusion(bf16[512,4096]{0,1:T(8,128)(2,1)} %copy-done.2, bf16[4096,512]{1,0:T(8,128)(2,1)} %all-gather.3.cloned.1.call-done), kind=kOutput, calls=%fused_computation.44 | convolution fusion | flops 2147745792 | bytes 8912896 | tf_op jit(solution)/shard_map/dot_general | solution.py:57
  168.6 41.5 %while.12 = (s32[]{:T(128)}, bf16[2,256,512]{2,1,0:T(8,128)(2,1)}, bf16[2,256,512]{2,1,0:T(8,128)(2,1)}, bf16[2,256,2048]{2,1,0:T(8,128)(2,1)}, s32[2]{0:T(128)S...) while((s32[]{:T(128)}, bf16[2,256,512]{2,1,0:T(8,128)(2,1)}, ...), condition=%wide.region_5.6_spmd, body=%wide.region_1.5_spmd.sunk | while | flops 1358427136 | bytes 69686040 | solution.py:75
  168.6 0.8 dynamic_slice.31
  169.4 0.7 iota_compare_fusion.3
  170.1 0.7 fusion.76
  171.1 1.0 constant_dynamic-slice_fusion.8
  172.0 0.8 copy.77
  172.9 1.3 constant_dynamic-slice_fusion.10
  174.2 0.5 copy.79
  174.7 1.3 constant_dynamic-slice_fusion.9
  176.5 4.4 fusion.74
  181.0 2.6 fusion.75
  183.6 0.8 fusion.77
  185.8 0.9 fusion.80
  186.7 0.8 fusion.81
  187.8 0.7 constant_dynamic-update-slice_fusion.3
  188.6 0.8 copy-done.7
  189.4 0.8 dynamic_slice.31
  190.2 0.7 iota_compare_fusion.3
  190.9 0.7 fusion.76
  191.8 1.0 constant_dynamic-slice_fusion.8
  192.8 0.8 copy.77
  193.7 1.3 constant_dynamic-slice_fusion.10
  194.9 0.5 copy.79
  195.5 1.3 constant_dynamic-slice_fusion.9
  197.3 4.4 fusion.74
  201.7 2.6 fusion.75
  204.4 0.8 fusion.77
  206.5 0.9 fusion.80
  207.5 0.8 fusion.81
  208.6 0.7 constant_dynamic-update-slice_fusion.3
  209.3 0.8 copy-done.7
  210.1 12.7 %fusion.27 = f32[4096,1024]{1,0:T(8,128)} fusion(bf16[512,4096]{0,1:T(8,128)(2,1)} %bitcast.135, bf16[512,512]{1,0:T(8,128)(2,1)} %bitcast.138, bf16[512,512]{1,0:T(8,128)(2,1)} %bitcast.139), kind=kOutput, calls=%fused_computation.45 | convolution fusion | flops 4297064448 | bytes 22020096 | tf_op jit(solution)/shard_map/dot_general | solution.py:44
  222.9 355.9 %reduce-scatter.2.cloned.1.call-done = f32[128,1024]{1,0:T(8,128)} async-done(((f32[4096,1024]{1,0:T(8,128)}), f32[128,1024]{1,0:T(8,128)}) %reduce-scatter.2.cloned.1.call-update) | async-done | bytes 524304 | tf_op jit(solution)/shard_map/reduce_scatter | solution.py:97
  578.8 2.0 multiply_reduce_fusion
  580.7 44.4 %psum.7 = f32[]{:T(128)} all-reduce(f32[]{:T(128)} %get-tuple-element.93), channel_id=1, replica_groups=mesh['replica'=2,'fsdp'=16] {'replica','fsdp'}, use_global_device_ids=true, to_apply=%region_8.9 | all-reduce | flops 1 | bytes 8 | tf_op jit(solution)/shard_map/psum | solution.py:100
  625.8 4.7 all_gather.11
  630.6 1.1 slice_multiply_fusion
  (51 shorter events, 5.4 us)
Async XLA Ops:
  7.2 77.8 %all-gather.5.cloned.1.call-start = ((), (), s32[]{:S(2)}) async-start(), calls=%async_computation.2 | async-start | bytes 4456448 | tf_op jit(solution)/shard_map/all_gather | solution.py:64
  9.0 153.0 %all-gather.3.cloned.1.call-start = ((), (), s32[]{:S(2)}) async-start(), calls=%async_computation.1 | async-start | bytes 4456448 | tf_op jit(solution)/shard_map/all_gather | solution.py:59
  10.9 567.9 %reduce-scatter.2.cloned.1.call-start = ((), (), s32[]{:S(2)}) async-start(), calls=%async_computation.3 | async-start | bytes 17301504 | tf_op jit(solution)/shard_map/reduce_scatter | solution.py:97
  10.9 9.8 %copy-start.5 = (f32[4096]{0:T(1024)S(1)}, f32[4096]{0:T(1024)}, u32[]{:S(2)}) copy-start(f32[4096]{0:T(1024)} %param.13) | copy-start | bytes 49156
  17.4 3.5 copy-start.1
  22.1 2.0 copy-start.2
  90.8 77.8 %copy-start.8 = (s32[2]{0:T(128)S(1)}, s32[2]{0:T(128)}, u32[]{:S(2)}) copy-start(s32[2]{0:T(128)} %param.12) | copy-start | bytes 28
  168.6 4.3 copy-start.3
  183.6 2.2 copy-start
  186.7 1.1 copy-start.6
  186.7 2.7 copy-start.4
  188.6 0.8 copy-start.7
  189.4 4.3 copy-start.3
  204.3 2.2 copy-start
  207.4 1.1 copy-start.6
  207.5 2.7 copy-start.4
  209.3 0.8 copy-start.7
Sparse Core Ops, SparseCore 0:
  10.7 74.2 all-gather.4
  87.8 74.1 all-gather.2
  223.0 355.6 reduce-scatter.1
where the time goes:
time: 639 us; the launch traced here: 638 us
  waiting for transfers between devices  486 us (76%)
  blocking collectives  49.1 us (8%)
  matrix products  39.9 us (6%)
  local copies, waits for them, and re-layouts  28.6 us (4%)
  other arithmetic  20 us (3%)
  between operations  14.5 us (2%)
    reduce_scatter x1, waiting for transfers between devices, local(): lax.psum_scatter(transposed_product(columns, combined), ('replica', 'fsdp...  356 us
    all_gather x1, waiting for transfers between devices, local(): lax.all_gather(key_master.astype(jnp.bfloat16), 'fsdp', axis=0, tiled=True)  71.2 us
    all_gather x1, waiting for transfers between devices, local(): lax.all_gather(value_master.astype(jnp.bfloat16), 'fsdp', axis=0, tiled=T...  58.6 us
    psum x1, blocking collectives, local(): total_sq = lax.psum(jnp.sum(owned_grad * owned_grad), ('replica', 'fsdp'))  44.4 us
    dynamic_slice x18, local copies, waits for them, and re-layouts, local(): lax.map(one_seq, (queries.reshape(seq_count, LEN, qwidth), key_proj.resha...  12.8 us
  transfers between devices with their start and end apart: 3, of which 3 were waited for; matrix products, arithmetic and copies ran while one was open for 3% of the time, Pallas kernels for 0%

commit v1 on v0

--- a/solution.py
+++ b/solution.py
@@ -8,6 +8,12 @@
 KVH = 4
 GROUP = 4
 LEN = 256
+change_record = lambda original: jnp.concatenate(
+    lax.all_to_all(
+        jnp.stack(lax.axis_size("fsdp") * [original]), axis_name="fsdp", split_axis=0, concat_axis=0
+    ),
+    axis=0,
+)
 
 
 def attend(query_seq, key_seq, value_seq, grad_seq, length):
@@ -55,9 +61,7 @@
     normed = (act_float * inverse * norm_gain[None, :]).astype(jnp.bfloat16)
     columns = normed
     key_sum = jnp.dot(
-        columns,
-        lax.all_gather(key_master.astype(jnp.bfloat16), "fsdp", axis=0, tiled=True),
-        preferred_element_type=jnp.float32,
+        columns, change_record(key_master.astype(jnp.bfloat16)), preferred_element_type=jnp.float32
     )
     value_sum = jnp.dot(
         columns,

time: 639 us -> 633 us (level)
  waiting for transfers between devices: 486 us -> 472 us
  starting transfers between devices: 0.12 us -> 6.9 us
    all_to_all x0 -> x1, waiting for transfers between devices: none -> 83 us  [lax.all_to_all(jnp.stack(lax.axis_size('fsdp') * [original]), axis_name='...]
    all_gather x1 -> x0, waiting for transfers between devices: 71.2 us -> none  [local(): lax.all_gather(key_master.astype(jnp.bfloat16), 'fsdp', axis=0, tiled=True)]
    all_gather x1, waiting for transfers between devices: 58.6 us -> 29 us  [local(): lax.all_gather(value_master.astype(jnp.bfloat16), 'fsdp', axis=0, tiled=T...]
    all_to_all x0 -> x1, starting transfers between devices: none -> 6.82 us  [lax.all_to_all(jnp.stack(lax.axis_size('fsdp') * [original]), axis_name='...]
where the time goes in v1:
time: 633 us; the launch traced here: 632 us
  waiting for transfers between devices  472 us (75%)
  blocking collectives  49 us (8%)
  matrix products  40.2 us (6%)
  local copies, waits for them, and re-layouts  30.7 us (5%)
  other arithmetic  18.2 us (3%)
  between operations  14.8 us (2%)
  starting transfers between devices  6.9 us (1%)
    reduce_scatter x1, waiting for transfers between devices, local(): lax.psum_scatter(transposed_product(columns, combined), ('replica', 'fsdp...  360 us
    all_to_all x1, waiting for transfers between devices, lax.all_to_all(jnp.stack(lax.axis_size('fsdp') * [original]), axis_name='...  83 us
    psum x1, blocking collectives, local(): total_sq = lax.psum(jnp.sum(owned_grad * owned_grad), ('replica', 'fsdp'))  44.3 us
    all_gather x1, waiting for transfers between devices, local(): lax.all_gather(value_master.astype(jnp.bfloat16), 'fsdp', axis=0, tiled=T...  29 us
    dot_general x1, matrix products, transposed_product(): lax.dot_general(columns, combined, (((0,), (0,)), ((), ())), preferred_el...  12.7 us
    dynamic_slice x18, local copies, waits for them, and re-layouts, local(): lax.map(one_seq, (queries.reshape(seq_count, LEN, qwidth), key_proj.resha...  12.7 us
  transfers between devices with their start and end apart: 3, of which 3 were waited for; matrix products, arithmetic and copies ran while one was open for 3% of the time, Pallas kernels for 0%

profile of v1, /device:TPU:7, one launch (start us, length us, event | category | flops | bytes accessed | tf_op | source)
XLA Modules:
  0.0 632.2 jit_solution(5360323428074929799)
XLA Ops:
  7.2 1.1 convert_element_type.72
  8.2 2.4 stack.2
  10.6 6.8 %all-to-all-start = ((bf16[16,256,512]{2,1,0:T(8,128)(2,1)}), bf16[16,256,512]{2,1,0:T(8,128)(2,1)}, u32[]{:S(2)}, u32[]{:S(2)}) async-start(bf16[16,256,512]{2,1,0:T(8,128)(2,1)} %stack.2), calls=%async_computation | async-start | bytes 8388608 | tf_op jit(solution)/shard_map/all_to_all | solution.py:12
  17.5 0.7 convert_element_type.74
  18.3 6.5 %copy.41 = bf16[512,4096]{0,1:T(8,128)(2,1)} copy(bf16[512,4096]{1,0:T(8,128)(2,1)} %param.9) | data formatting | bytes 8388608 | tf_op args[0]
  24.8 3.3 fusion.24
  28.3 1.1 fusion.26
  29.4 1.9 copy-done.2
  31.3 2.4 copy.42
  33.7 83.0 %all-to-all-done = bf16[16,256,512]{2,1,0:T(8,128)(2,1)} async-done(((bf16[16,256,512]{2,1,0:T(8,128)(2,1)}), bf16[16,256,512]{2,1,0:T(8,128)(2,1)}, u32[]{:S(2)}, u32[]{:S(2)}) %all-to-all-start) | async-done | bytes 4194336 | tf_op jit(solution)/shard_map/all_to_all | solution.py:12
  116.7 6.1 convolution_convert_fusion.2
  122.9 29.0 %all-gather.2.cloned.1.call-done = bf16[4096,512]{1,0:T(8,128)(2,1)} async-done(((bf16[256,512]{1,0:T(8,128)(2,1)}), bf16[4096,512]{1,0:T(8,128)(2,1)}) %all-gather.2.cloned.1.call-update) | async-done | bytes 4194320 | tf_op jit(solution)/shard_map/all_gather | solution.py:68
  151.9 6.6 %convolution_convert_fusion.1 = bf16[512,512]{1,0:T(8,128)(2,1)} fusion(bf16[512,4096]{0,1:T(8,128)(2,1)} %copy-done.2, bf16[4096,512]{1,0:T(8,128)(2,1)} %all-gather.2.cloned.1.call-done), kind=kOutput, calls=%fused_computation.43 | convolution fusion | flops 2147745792 | bytes 8912896 | tf_op jit(solution)/shard_map/dot_general | solution.py:66
  158.5 41.4 %while.12 = (s32[]{:T(128)}, bf16[2,256,512]{2,1,0:T(8,128)(2,1)}, bf16[2,256,512]{2,1,0:T(8,128)(2,1)}, bf16[2,256,2048]{2,1,0:T(8,128)(2,1)}, s32[2]{0:T(128)S...) while((s32[]{:T(128)}, bf16[2,256,512]{2,1,0:T(8,128)(2,1)}, ...), condition=%wide.region_5.6_spmd, body=%wide.region_1.5_spmd.sunk | while | flops 1358427136 | bytes 69686040 | solution.py:79
  158.5 0.7 dynamic_slice.31
  159.3 0.7 iota_compare_fusion.3
  159.9 0.7 fusion.76
  160.7 1.0 constant_dynamic-slice_fusion.11
  161.9 0.8 copy.77
  162.7 1.3 constant_dynamic-slice_fusion.10
  164.6 1.3 constant_dynamic-slice_fusion.9
  166.4 4.4 fusion.74
  170.8 2.6 fusion.75
  173.4 0.8 fusion.77
  175.6 0.9 fusion.80
  176.5 0.8 fusion.81
  177.6 0.7 constant_dynamic-update-slice_fusion.3
  178.4 0.8 copy-done.8
  179.2 0.7 dynamic_slice.31
  179.9 0.7 iota_compare_fusion.3
  180.6 0.7 fusion.76
  181.4 1.0 constant_dynamic-slice_fusion.11
  182.5 0.8 copy.77
  183.4 1.3 constant_dynamic-slice_fusion.10
  185.2 1.3 constant_dynamic-slice_fusion.9
  187.1 4.4 fusion.74
  191.5 2.6 fusion.75
  194.1 0.8 fusion.77
  196.3 0.9 fusion.80
  197.2 0.8 fusion.81
  198.3 0.7 constant_dynamic-update-slice_fusion.3
  199.1 0.8 copy-done.8
  199.9 12.7 %fusion.27 = f32[4096,1024]{1,0:T(8,128)} fusion(bf16[512,4096]{0,1:T(8,128)(2,1)} %bitcast.136, bf16[512,512]{1,0:T(8,128)(2,1)} %bitcast.139, bf16[512,512]{1,0:T(8,128)(2,1)} %bitcast.140), kind=kOutput, calls=%fused_computation.45 | convolution fusion | flops 4297064448 | bytes 22020096 | tf_op jit(solution)/shard_map/dot_general | solution.py:50
  212.6 359.8 %reduce-scatter.2.cloned.1.call-done = f32[128,1024]{1,0:T(8,128)} async-done(((f32[4096,1024]{1,0:T(8,128)}), f32[128,1024]{1,0:T(8,128)}) %reduce-scatter.2.cloned.1.call-update) | async-done | bytes 524304 | tf_op jit(solution)/shard_map/reduce_scatter | solution.py:101
  572.4 2.0 multiply_reduce_fusion
  574.4 44.3 %psum.7 = f32[]{:T(128)} all-reduce(f32[]{:T(128)} %get-tuple-element.93), channel_id=1, replica_groups=mesh['replica'=2,'fsdp'=16] {'replica','fsdp'}, use_global_device_ids=true, to_apply=%region_8.9 | all-reduce | flops 1 | bytes 8 | tf_op jit(solution)/shard_map/psum | solution.py:104
  619.4 4.7 all_gather.7
  624.2 1.1 slice_multiply_fusion
  (53 shorter events, 6.3 us)
Async XLA Ops:
  10.6 6.9 %copy-start.5 = (f32[256,512]{1,0:T(8,128)S(1)}, f32[256,512]{1,0:T(8,128)}, u32[]{:S(2)}) copy-start(f32[256,512]{1,0:T(8,128)} %param.15) | copy-start | bytes 1572868
  10.6 106.1 %all-to-all-start = ((bf16[16,256,512]{2,1,0:T(8,128)(2,1)}), bf16[16,256,512]{2,1,0:T(8,128)(2,1)}, u32[]{:S(2)}, u32[]{:S(2)}) async-start(bf16[16,256,512]{2,1,0:T(8,128)(2,1)} %stack.2), calls=%async_computation | async-start | bytes 8388608 | tf_op jit(solution)/shard_map/all_to_all | solution.py:12
  17.4 134.5 %all-gather.2.cloned.1.call-start = ((), (), s32[]{:S(2)}) async-start(), calls=%async_computation.2 | async-start | bytes 4456448 | tf_op jit(solution)/shard_map/all_gather | solution.py:68
  18.2 554.2 %reduce-scatter.2.cloned.1.call-start = ((), (), s32[]{:S(2)}) async-start(), calls=%async_computation.3 | async-start | bytes 17301504 | tf_op jit(solution)/shard_map/reduce_scatter | solution.py:101
  18.3 9.8 %copy-start.6 = (f32[4096]{0:T(1024)S(1)}, f32[4096]{0:T(1024)}, u32[]{:S(2)}) copy-start(f32[4096]{0:T(1024)} %param.13) | copy-start | bytes 49156
  24.8 3.4 copy-start.1
  29.3 1.9 copy-start.2
  122.9 35.6 %copy-start.9 = (s32[2]{0:T(128)S(1)}, s32[2]{0:T(128)}, u32[]{:S(2)}) copy-start(s32[2]{0:T(128)} %param.12) | copy-start | bytes 28
  158.5 4.2 copy-start.3
  173.4 2.2 copy-start
  176.5 1.1 copy-start.7
  176.5 2.7 copy-start.4
  178.4 0.8 copy-start.8
  179.2 4.2 copy-start.3
  194.1 2.2 copy-start
  197.2 1.1 copy-start.7
  197.2 2.7 copy-start.4
  199.1 0.8 copy-start.8
Sparse Core Ops, SparseCore 0:
  21.0 130.8 all-gather.1
  212.7 359.6 reduce-scatter.1
